TPU v7x, 32 devices: a whole 2x2x4 slice. The times are simulated.
32 devices in a mesh: seq: 8 (over z, y), mp: 4 (over x, core).
Axes of the slice: x: 2, y: 2, z: 4, core: 2. Of those that a mesh axis runs over, the one named last changes fastest.
Arguments:
- ssm_input: bfloat16 [8192, 5120], P('seq', 'mp'), may hold values from -6 to 6
- gate_input: bfloat16 [8192, 5120], P('seq', 'mp'), may hold values from -6 to 6
- state_in: bfloat16 [8192, 128], P('seq'), may hold values from -6 to 6
- state_out: bfloat16 [8192, 128], P('seq'), may hold values from -0.5 to 0.5
- step_size: float32 [8192, 80], P('seq', 'mp'), may hold values from 0.05 to 0.2
- log_decay: float32 [8192, 80], P('seq', 'mp'), may hold values from -2 to 0
- skip_gain: float32 [80], P('mp'), may hold values from 0.5 to 2
- norm_gain: bfloat16 [5120], P('mp'), may hold values from 0.099609375 to 1.8984375
- out_weight: bfloat16 [5120, 2560], P('mp'), may hold values from -0.078125 to 0.078125
Outputs:
- layer_out: bfloat16 [8192, 2560], P(('seq', 'mp'))
All inputs are finite; a program needn't handle non-finite values.
Results may differ from a plain program's by a relative error of at most 0.011.
Values may be sent and summed in bfloat16 or wider, within the bound.
A program may use at most 64 MiB of HBM per device.

v0:
```python
import jax
import jax.numpy as jnp
from jax import lax
from jax.sharding import PartitionSpec as P

BLOCK = 256


def carried_in(value, axis, combine, identity):
    size, place = (lax.axis_size(axis), lax.axis_index(axis))
    everything = jax.tree.map(lambda part: lax.all_gather(part, axis), value)
    start = jax.tree.map(
        lambda part, zero: jnp.broadcast_to(jnp.asarray(zero, part.dtype), part.shape),
        value,
        identity,
    )

    def hop(k, before):
        reached = k < place
        new = combine(before, jax.tree.map(lambda part: part[k], everything))
        return jax.tree.map(lambda a, b: jnp.where(reached, a, b), new, before)

    return lax.fori_loop(0, size, hop, start)


def combine(earlier, later):
    return (earlier[0] * later[0], later[0][:, None, None] * earlier[1] + later[1])


def body(
    ssm_input,
    gate_input,
    state_in,
    state_out,
    step_size,
    log_decay,
    skip_gain,
    norm_gain,
    out_weight,
):
    tok_rows = ssm_input.shape[0]
    head_count = step_size.shape[1]
    channels = ssm_input.shape[1]
    head_width = channels // head_count
    blocks = tok_rows // BLOCK
    inputs = ssm_input.reshape(blocks, BLOCK, head_count, head_width)
    writers = state_in.reshape(blocks, BLOCK, state_in.shape[1])
    readers = state_out.reshape(blocks, BLOCK, state_out.shape[1])
    steps_blk = step_size.reshape(blocks, BLOCK, head_count)
    level = jnp.cumsum(log_decay.reshape(blocks, BLOCK, head_count), axis=1)
    closing = level[:, -1, :]
    weighted = (
        (jnp.exp(closing[:, None, :] - level) * steps_blk)[..., None] * inputs.astype(jnp.float32)
    ).astype(jnp.bfloat16)
    own_states = jnp.einsum("kshp,ksn->khpn", weighted, writers, preferred_element_type=jnp.float32)
    block_decay = jnp.exp(closing)
    running = jnp.zeros(own_states.shape[1:], jnp.float32)
    earlier_list = []
    for index in range(blocks):
        earlier_list.append(running)
        running = block_decay[index][:, None, None] * running + own_states[index]
    leading = jnp.exp(jnp.cumsum(closing, axis=0) - closing)
    device_decay = jnp.exp(jnp.sum(closing, axis=0))
    identity = (jnp.ones_like(device_decay), jnp.zeros_like(running))
    prefix = carried_in((device_decay, running), "seq", combine, identity)
    carried = jnp.stack(earlier_list) + leading[:, :, None, None] * prefix[1][None]
    from_carry = jnp.exp(level)[..., None] * jnp.einsum(
        "kln,khpn->klhp", readers.astype(jnp.float32), carried, precision=lax.Precision.HIGHEST
    )
    intersections = jnp.einsum("ktn,ksn->kts", readers, writers, preferred_element_type=jnp.float32)
    causal = (jnp.arange(BLOCK)[:, None] >= jnp.arange(BLOCK)[None, :])[None, None]
    level_t = jnp.transpose(level, (0, 2, 1))
    gaps = level_t[:, :, :, None] - level_t[:, :, None, :]
    decays = jnp.where(causal, jnp.exp(jnp.where(causal, gaps, 0.0)), 0.0)
    scores = (
        decays * intersections[:, None] * jnp.transpose(steps_blk, (0, 2, 1))[:, :, None, :]
    ).astype(jnp.bfloat16)
    within = jnp.einsum("khts,kshp->kthp", scores, inputs, preferred_element_type=jnp.float32)
    mixed = within + from_carry + skip_gain[None, None, :, None] * inputs.astype(jnp.float32)
    gated = mixed.reshape(tok_rows, channels) * jax.nn.silu(gate_input.astype(jnp.float32))
    group = lax.axis_size("mp")
    square_total = lax.psum(jnp.sum(gated * gated, axis=1), "mp")
    scale = lax.rsqrt(square_total / (channels * group) + 1e-05)
    normed = (gated * scale[:, None] * norm_gain.astype(jnp.float32)[None, :]).astype(jnp.bfloat16)
    layer_out = lax.psum_scatter(
        jnp.dot(normed, out_weight, preferred_element_type=jnp.float32),
        "mp",
        scatter_dimension=0,
        tiled=True,
    )
    return layer_out.astype(jnp.bfloat16)


def solution(mesh):
    placed = (
        P("seq", "mp"),
        P("seq", "mp"),
        P("seq", None),
        P("seq", None),
        P("seq", "mp"),
        P("seq", "mp"),
        P("mp"),
        P("mp"),
        P("mp", None),
    )
    return jax.shard_map(
        body, mesh=mesh, in_specs=placed, out_specs=P(("seq", "mp"), None), check_vma=False
    )
```

profile of v0, /device:TPU:29, one launch (start us, length us, event | category | flops | bytes accessed | tf_op | source)
XLA Modules:
  0.0 253.4 jit_solution(5920171022278220565)
XLA Ops:
  6.5 0.0 copy-start
  6.5 0.0 all-gather.3.cloned.1.call-start
  6.5 1.0 reshape.97
  7.5 0.1 reshape.98
  7.6 2.3 reduce-window.6
  9.9 0.1 slice.44
  10.0 0.1 copy.33
  10.2 0.1 broadcast_add_fusion
  10.3 0.1 reduce_window_sum.35
  10.4 0.3 slice_reduce_fusion
  10.7 0.1 copy.42
  10.9 0.1 copy.43
  11.0 0.9 reshape.102
  11.9 0.1 bitcast_exponential_fusion.1
  12.1 0.0 copy-start.5
  12.1 3.0 %copy.39 = bf16[1024,1280]{0,1:T(8,128)(2,1)S(1)} copy(bf16[1024,1280]{1,0:T(8,128)(2,1)} %param.11) | data formatting | bytes 5242880 | tf_op args[0]
  15.1 3.5 %reshape.103 = bf16[4,256,20,64]{1,0,3,2:T(4,128)(2,1)} reshape(bf16[1024,1280]{0,1:T(8,128)(2,1)S(1)} %copy.39) | data formatting | bytes 5242880 | tf_op jit(solution)/shard_map/reshape | solution.py:46
  18.7 0.0 copy-done.5
  18.7 2.6 %fusion.16 = f32[4,20,64,128]{3,2,1,0:T(8,128)S(1)} fusion(bf16[4,256,128,1]{2,1,3,0:T(8,128)(2,1)S(1)} %bitcast.78, f32[4,256,20]{1,2,0:T(8,128)S(1)} %copy.44, bf16[4,256,20,64]{1,0,3,2:T(4,128)(2,1)} %reshape.103), kind=kOutput, calls=%fused_computation.26 | convolution fusion | flops 339476480 | bytes 5586944 | tf_op jit(solution)/shard_map/kshp,ksn->khpn/dot_general | solution.py:55
  21.3 0.0 copy-start.10
  21.3 0.0 copy-start.12
  21.3 1.8 slice_add_fusion
  23.1 0.0 all-gather.3.cloned.1.call-update
  23.1 0.0 reduce-scatter.2.cloned.1.call-start
  23.2 0.7 copy.36
  23.8 0.0 copy-done.10
  23.8 0.0 copy-done.12
  23.8 0.6 dynamic-slice
  25.1 0.1 exponential_dynamic-update-slice_fusion
  25.2 13.9 %all-reduce = f32[160]{0:T(256)S(1)} all-reduce(f32[160]{0:T(256)S(1)} %exponential_dynamic-update-slice_fusion), channel_id=2, replica_groups=mesh['seq'=8,'mp'=4] {'seq'}, use_global_device_ids=true, to_apply=%add | all-reduce | flops 160 | bytes 1280
  39.1 0.1 reshape.105
  39.2 0.7 copy.41
  39.9 0.7 copy.38
  40.5 3.0 %copy.47 = bf16[1024,1280]{0,1:T(8,128)(2,1)S(1)} copy(bf16[1024,1280]{1,0:T(8,128)(2,1)} %param.12) | data formatting | bytes 5242880 | tf_op args[1]
  43.5 0.5 pad.clone
  44.0 0.6 iota_compare_fusion
  44.7 0.0 copy-done
  44.7 2.2 fusion.38
  46.9 60.6 %all-gather.3.cloned.1.call-done = f32[8,20,64,128]{3,2,1,0:T(8,128)} async-done(((f32[1,20,64,128]{3,2,1,0:T(8,128)}), f32[8,20,64,128]{3,2,1,0:T(8,128)}) %all-gather.3.cloned.1.call-update) | async-done | bytes 5242896 | tf_op jit(solution)/shard_map/all_gather | solution.py:11
  107.5 10.2 %while.14 = (s32[]{:T(128)}, f32[20,64,128]{2,1,0:T(8,128)S(1)}, s32[]{:T(128)}, f32[8,20]{1,0:T(8,128)S(1)}, f32[8,20,64,128]{3,2,1,0:T(8,128)}, /*index=5*/s32[]{:T(128)}, s32[]{:T(128)}) while((s32[]{:T(128)}, f32[20,64,128]{2,1,0:T(8,128)S(1)}, s32[]{:T(128)}, f32[8,20]{1,0:T(8,128)S(1)}, f32[8,20,64,128]{3,2,1,0:T(8,128)}, ...), condition=%wide.region_5.6_spmd.clone, body=%wide.region_4.5_spmd.clone.sunk | while | flops 655364 | bytes 1966433 | solution.py:23
  107.6 1.2 fusion.45
  108.8 1.2 fusion.45
  110.1 1.2 fusion.45
  111.4 1.2 fusion.45
  112.6 1.2 fusion.45
  113.9 1.2 fusion.45
  115.2 1.2 fusion.45
  116.5 1.2 fusion.45
  117.7 0.0 copy-start.3
  117.7 0.0 copy-start.4
  117.7 0.0 copy-start.6
  117.8 0.0 copy-start.11
  117.8 3.9 %fusion.18 = f32[4,20,64,256]{3,2,1,0:T(8,128)S(1)} fusion(bf16[4,256,128,1]{2,1,3,0:T(8,128)(2,1)S(1)} %bitcast.69, f32[1,20,64,128]{3,2,1,0:T(8,128)} %get-tuple-element.129, f32[1,20,64,128]{3,2,1,0:T(8,128)} %get-tuple-element.130, f32[1,20,64,128]{3,2,1,0:T(8,128)} %get-tuple-element.131, f32[4]{0:T(128)} %pad.clone, ...), kind=kOutput, calls=%fused_computation.28 | convolution fusion | flops 2016542720 | bytes 8126800 | tf_op jit(solution)/shard_map/kln,khpn->klhp/dot_general | solution.py:67
  121.8 7.4 %fusion.9 = f32[4,256,20,64]{1,3,2,0:T(8,128)S(1)} fusion(f32[4,20,64,256]{3,2,1,0:T(8,128)S(1)} %fusion.18, f32[20]{0:T(128)S(1)} %copy-done.11, f32[4,256,20]{1,2,0:T(8,128)S(1)} %copy-done.7, f32[4,20,256]{2,1,0:T(8,128)S(1)} %copy-done.8, f32[4,256,256]{2,1,0:T(8,128)S(1)} %copy-done.4, f32[4,20,256]{2,1,0:T(8,128)S(1)} %copy-done.6, ...), kind=kOutput, calls=%fused_computation.16 | convolution fusion | flops 709099520 | bytes 14467152 | tf_op jit(solution)/shard_map/khts,kshp->kthp/dot_general | solution.py:78
  129.2 3.9 %copy.46 = f32[4,256,20,64]{1,0,3,2:T(4,128)S(1)} copy(f32[4,256,20,64]{1,3,2,0:T(8,128)S(1)} %fusion.9) | data formatting | bytes 10485760 | tf_op jit(solution)/shard_map/add | solution.py:79
  133.1 1.3 copy.50
  134.4 0.0 copy-start.2
  134.4 2.4 copy-done.2
  136.8 1.8 multiply_reduce_fusion
  138.6 5.7 %psum.7 = f32[1024]{0:T(1024)S(1)} all-reduce(f32[1024]{0:T(1024)S(1)} %multiply_reduce_fusion), channel_id=1, replica_groups=mesh['seq'=8,'mp'=4] {'mp'}, use_global_device_ids=true, to_apply=%region_7.8 | all-reduce | flops 1024 | bytes 8192 | tf_op jit(solution)/shard_map/psum | solution.py:82
  144.2 13.8 %fusion.15 = f32[1024,2560]{1,0:T(8,128)} fusion(bf16[1280,2560]{1,0:T(8,128)(2,1)} %param.19, f32[1280]{0:T(1024)S(1)} %convert_element_type.27, f32[1024]{0:T(1024)S(1)} %add_rsqrt_fusion, f32[1024,1280]{0,1:T(8,128)} %bitcast.72, bf16[1024,1280]{0,1:T(8,128)(2,1)S(1)} %copy.47), kind=kOutput, calls=%fused_computation.25 | convolution fusion | flops 6722682880 | bytes 24912896 | tf_op jit(solution)/shard_map/dot_general | solution.py:86
  158.0 0.0 reduce-scatter.2.cloned.1.call-update
  158.1 85.6 %reduce-scatter.2.cloned.1.call-done = f32[256,2560]{1,0:T(8,128)} async-done(((f32[1024,2560]{1,0:T(8,128)}), f32[256,2560]{1,0:T(8,128)}) %reduce-scatter.2.cloned.1.call-update) | async-done | bytes 2621456 | tf_op jit(solution)/shard_map/reduce_scatter | solution.py:85
  243.7 2.9 %convert_element_type.29 = bf16[256,2560]{1,0:T(8,128)(2,1)} convert(f32[256,2560]{1,0:T(8,128)} %reduce-scatter.2.cloned.1.call-done) | non-fusion elementwise | flops 655360 | bytes 3932160 | tf_op jit(solution)/shard_map/convert_element_type | solution.py:91
  (33 shorter events, 0.2 us)
Async XLA Ops:
  6.5 38.1 %copy-start = (bf16[1024,128]{1,0:T(8,128)(2,1)S(1)}, bf16[1024,128]{1,0:T(8,128)(2,1)}, u32[]{:S(2)}) copy-start(bf16[1024,128]{1,0:T(8,128)(2,1)} %param.14) | copy-start | bytes 786436
  6.5 101.0 %all-gather.3.cloned.1.call-start = ((), (), s32[]{:S(2)}) async-start(), calls=%async_computation.1 | async-start | bytes 5898240 | tf_op jit(solution)/shard_map/all_gather | solution.py:11
  12.1 6.6 %copy-start.5 = (bf16[1024,128]{1,0:T(8,128)(2,1)S(1)}, bf16[1024,128]{1,0:T(8,128)(2,1)}, u32[]{:S(2)}) copy-start(bf16[1024,128]{1,0:T(8,128)(2,1)} %param.13) | copy-start | bytes 786436
  21.3 2.5 %copy-start.10 = (bf16[1280]{0:T(1024)(128)(2,1)S(1)}, bf16[1280]{0:T(1024)(128)(2,1)}, u32[]{:S(2)}) copy-start(bf16[1280]{0:T(1024)(128)(2,1)} %param.18) | copy-start | bytes 7684
  21.3 2.5 %copy-start.12 = (u32[32]{0:T(128)S(1)}, u32[32]{0:T(128)}, u32[]{:S(2)}) copy-start(u32[32]{0:T(128)} %constant.50) | copy-start | bytes 388
  23.1 220.5 %reduce-scatter.2.cloned.1.call-start = ((), (), s32[]{:S(2)}) async-start(), calls=%async_computation.2 | async-start | bytes 13107200 | tf_op jit(solution)/shard_map/reduce_scatter | solution.py:85
  117.7 4.0 %copy-start.3 = (bf16[4,256,20,64]{1,0,3,2:T(4,128)(2,1)S(1)}, bf16[4,256,20,64]{1,0,3,2:T(4,128)(2,1)}, u32[]{:S(2)}) copy-start(bf16[4,256,20,64]{1,0,3,2:T(4,128)(2,1)} %reshape.103) | copy-start | bytes 7864324
  117.7 4.0 %copy-start.4 = (f32[4,256,256]{2,1,0:T(8,128)S(1)}, f32[4,256,256]{2,1,0:T(8,128)}, u32[]{:S(2)}) copy-start(f32[4,256,256]{2,1,0:T(8,128)} %fusion.38) | copy-start | bytes 3145732
  117.7 4.0 %copy-start.6 = (f32[4,20,256]{2,1,0:T(8,128)S(1)}, f32[4,20,256]{2,1,0:T(8,128)}, u32[]{:S(2)}) copy-start(f32[4,20,256]{2,1,0:T(8,128)} %copy.36) | copy-start | bytes 245764
  117.8 4.0 %copy-start.7 = (f32[4,256,20]{1,2,0:T(8,128)S(1)}, f32[4,256,20]{1,2,0:T(8,128)}, u32[]{:S(2)}) copy-start(f32[4,256,20]{1,2,0:T(8,128)} %copy.41) | copy-start | bytes 245764
  117.8 4.0 %copy-start.8 = (f32[4,20,256]{2,1,0:T(8,128)S(1)}, f32[4,20,256]{2,1,0:T(8,128)}, u32[]{:S(2)}) copy-start(f32[4,20,256]{2,1,0:T(8,128)} %copy.38) | copy-start | bytes 245764
  117.8 4.0 %copy-start.9 = (pred[256,256]{1,0:T(8,128)(4,1)S(1)}, pred[256,256]{1,0:T(8,128)(4,1)}, u32[]{:S(2)}) copy-start(pred[256,256]{1,0:T(8,128)(4,1)} %iota_compare_fusion) | copy-start | bytes 196612
  117.8 4.0 %copy-start.11 = (f32[20]{0:T(128)S(1)}, f32[20]{0:T(128)}, u32[]{:S(2)}) copy-start(f32[20]{0:T(128)} %param.17) | copy-start | bytes 244
  134.4 2.4 copy-start.2
  158.0 88.5 %copy-start.1 = (bf16[1024,128]{1,0:T(8,128)(2,1)S(1)}, bf16[1024,128]{1,0:T(8,128)(2,1)}, u32[]{:S(2)}) copy-start(bf16[1024,128]{1,0:T(8,128)(2,1)} %param.14) | copy-start | bytes 786436
Sparse Core Ops, SparseCore 0:
  23.2 84.2 all-gather.2
  158.2 85.4 reduce-scatter.1
where the time goes:
time: 256 us; the launch traced here: 253 us
  waiting for transfers between devices  146 us (57%)
  matrix products  29.9 us (12%)
  local copies, waits for them, and re-layouts  23.1 us (9%)
  other arithmetic  19.9 us (8%)
  blocking collectives  19.6 us (8%)
  between operations  14.4 us (6%)
    reduce_scatter x1, waiting for transfers between devices, body(): lax.psum_scatter(jnp.dot(normed, out_weight, preferred_element_type=jnp.f...  85.6 us
    all_gather x1, waiting for transfers between devices, carried_in(): everything = jax.tree.map(lambda part: lax.all_gather(part, axis), value)  60.6 us
    unnamed x1, blocking collectives  13.9 us
    dot_general x1, matrix products, body(): jnp.dot(normed, out_weight, preferred_element_type=jnp.float32)  13.8 us
    unnamed x32, local copies, waits for them, and re-layouts  10.4 us
    select_n x8, other arithmetic, hop(): return jax.tree.map(lambda a, b: jnp.where(reached, a, b), new, before)  9.88 us
    dot_general x1, matrix products, body(): jnp.einsum('khts,kshp->kthp', scores, inputs, preferred_element_type=jnp....  7.42 us
    psum x1, blocking collectives, body(): square_total = lax.psum(jnp.sum(gated * gated, axis=1), 'mp')  5.67 us
  transfers between devices with their start and end apart: 2, of which 2 were waited for; matrix products, arithmetic and copies ran while one was open for 4% of the time, Pallas kernels for 0%

commit v1 on v0

v1 whole, which is shorter than its diff:
```python
import functools

import jax
import jax.numpy as jnp
from jax import lax
from jax.experimental import pallas as pl
from jax.experimental.pallas import tpu as pltpu
from jax.sharding import PartitionSpec as P

BLOCK = 256
LOG2E = 1.4426950408889634
HI = lax.Precision.HIGHEST
F32 = jnp.float32
BF16 = jnp.bfloat16


def dotg(a, b, ca, cb, precision=None):
    return lax.dot_general(
        a, b, (((ca,), (cb,)), ((), ())), preferred_element_type=F32, precision=precision
    )


def kernel(
    cfg, x_ref, gate_hbm, b_ref, c_ref, stp_ref, ldt_ref, skip_ref, gain_ref, w_hbm,
    out_ref,
    gate, w, lev, lvs, levt, pref, lead, total, y, sg, u, ss,
    csend, crecv, psend, precv, xsend, xrecv, acc, ssrecv,
    load_sem, cs_sem, cr_sem, ps_sem, pr_sem, xs_sem, xr_sem, ss_sem, sr_sem,
):
    S, n, tok, ch, heads, D, cw, dc = cfg
    X, rd, blocks = n // 2, tok // n, tok // BLOCK
    hw = ch // heads
    per = 128 // hw
    pieces, nc = ch // 128, D // dc
    rows_chip = tok // X
    s, m = lax.axis_index("seq"), lax.axis_index("mp")
    chip, core = m // 2, lax.rem(m, 2)
    peer = chip * 2 + 1 - core

    load_gate = pltpu.make_async_copy(gate_hbm, gate, load_sem.at[0])
    load_w = pltpu.make_async_copy(w_hbm, w, load_sem.at[1])
    load_gate.start()
    load_w.start()

    barrier = pltpu.get_barrier_semaphore()
    for o in range(1, n):
        pl.semaphore_signal(barrier, inc=1, device_id={"mp": lax.rem(m + o, n)})
    for o in (1, S - 1):
        pl.semaphore_signal(barrier, inc=1, device_id={"seq": lax.rem(s + o, S)})
    pl.semaphore_wait(barrier, n + 1)

    spread = (
        lax.broadcasted_iota(jnp.int32, (heads, ch), 1) // hw
        == lax.broadcasted_iota(jnp.int32, (heads, ch), 0)
    )
    spread32, spread16 = spread.astype(F32), spread.astype(BF16)
    ti = lax.broadcasted_iota(jnp.int32, (BLOCK, BLOCK), 0)
    si = lax.broadcasted_iota(jnp.int32, (BLOCK, BLOCK), 1)
    tril = (ti >= si).astype(F32)
    triu = (ti <= si).astype(F32)
    eye = (ti == si).astype(F32)

    total[...] = jnp.zeros_like(total)
    ones = jnp.ones((8, ch), F32)

    def states(k, _):
        rows = pl.ds(pl.multiple_of(k * BLOCK, BLOCK), BLOCK)
        ldt = ldt_ref[:, rows] * LOG2E
        lst = jnp.log2(stp_ref[:, rows])
        level = dotg(tril, ldt, 1, 1, HI)
        shifted = level - dotg(eye, lst, 1, 1, HI)
        lev[rows, :] = level
        levt[k] = dotg(ldt, triu, 1, 0, HI) - lst
        closing = level[BLOCK - 1 : BLOCK, :]
        fac = jnp.exp2(closing - shifted).astype(BF16)
        decay = dotg(
            jnp.broadcast_to(jnp.exp2(closing), (8, heads)), spread32, 1, 0, HI
        )
        for j in range(ch // cw):
            cols = slice(j * cw, (j + 1) * cw)
            wide = dotg(fac, spread16[:, cols], 1, 0)
            weighted = (wide * x_ref[rows, cols].astype(F32)).astype(BF16)
            own = dotg(b_ref[rows, :], weighted, 0, 0)
            now = total[:, cols]
            pref[k, :, cols] = now
            total[:, cols] = decay[0:1, cols] * now + own
        before = jnp.where(k == 0, ones, lead[k])
        lead[k] = before
        lead[k + 1] = before * decay
        return 0

    lead[0] = ones
    lax.fori_loop(0, blocks, states, 0)

    def chain_copy(j):
        cols = pl.ds(pl.multiple_of(j * 128, 128), 128)
        return pltpu.make_async_remote_copy(
            src_ref=csend.at[j],
            dst_ref=crecv.at[j],
            send_sem=cs_sem.at[j],
            recv_sem=cr_sem.at[j],
            device_id={"seq": lax.rem(s + 1, S)},
        ), cols

    def chain(j, _):
        copy, cols = chain_copy(j)

        @pl.when(s == 0)
        def _():
            crecv[j] = jnp.zeros(crecv.shape[1:], BF16)

        @pl.when(s > 0)
        def _():
            copy.wait_recv()

        @pl.when(s < S - 1)
        def _():
            after = lead[blocks, 0:1, cols] * crecv[j].astype(F32) + total[:, cols]
            csend[j] = after.astype(BF16)
            copy.start()

        return 0

    load_gate.wait()
    lane = lax.broadcasted_iota(jnp.int32, (BLOCK, 128), 1)
    skip = dotg(jnp.broadcast_to(skip_ref[...], (8, heads)), spread32, 1, 0, HI)
    half = BLOCK // 2

    def within(k, _):
        @pl.when(k == (s * blocks) // S)
        def _():
            lax.fori_loop(0, pieces, chain, 0)

        rows = pl.ds(pl.multiple_of(k * BLOCK, BLOCK), BLOCK)
        inter = jnp.where(ti >= si, dotg(c_ref[rows, :], b_ref[rows, :], 1, 1), 0.0)
        top, low = inter[:half, :half], inter[half:, :]
        level = lev[rows, :]
        for q in range(pieces):
            cols = slice(q * 128, (q + 1) * 128)
            xp = x_ref[rows, cols]
            mix = skip[0:1, cols] * xp.astype(F32)
            res = None
            for p in range(per):
                h = q * per + p
                lt = level[:, h : h + 1]
                ls = levt[k, h : h + 1, :]
                g0 = jnp.exp2(jnp.minimum(lt[:half] - ls[:, :half], 0.0)) * top
                g1 = jnp.exp2(jnp.minimum(lt[half:] - ls, 0.0)) * low
                r = jnp.concatenate(
                    [dotg(g0.astype(BF16), xp[:half], 1, 0), dotg(g1.astype(BF16), xp, 1, 0)],
                    axis=0,
                )
                res = r if res is None else jnp.where(lane < p * hw, res, r)
            y[rows, cols] = mix + res
            v = gate[rows, cols].astype(F32)
            sg[rows, cols] = (v / (1.0 + jnp.exp(-v))).astype(BF16)
        return 0

    lax.fori_loop(0, blocks, within, 0)
    load_w.wait()

    def to_peer(i, j):
        return pltpu.make_async_remote_copy(
            src_ref=psend.at[i, j], dst_ref=precv.at[i, j],
            send_sem=ps_sem.at[i, j], recv_sem=pr_sem.at[i, j],
            device_id={"mp": peer},
        )

    def to_chip(i, j):
        return pltpu.make_async_remote_copy(
            src_ref=xsend.at[i, j], dst_ref=xrecv.at[i, j],
            send_sem=xs_sem.at[i, j], recv_sem=xr_sem.at[i, j],
            device_id={"mp": lax.rem(chip + 1 + i, X) * 2 + core},
        )

    def ss_copy(o):
        t = lax.rem(m + o, n)
        return pltpu.make_async_remote_copy(
            src_ref=ss.at[t], dst_ref=ssrecv.at[o],
            send_sem=ss_sem.at[o], recv_sem=sr_sem.at[o],
            device_id={"mp": t},
        )

    unit = jnp.ones((8, cw), BF16)
    gaincols = gain_ref[...].astype(F32)

    def gating(r0):
        k = r0 // BLOCK
        rows = pl.ds(pl.multiple_of(r0, BLOCK), BLOCK)
        grow = jnp.exp2(lev[rows, :]).astype(BF16)
        reader = c_ref[rows, :]
        sq = jnp.zeros((8, BLOCK), F32)
        for j in range(ch // cw):
            cols = slice(j * cw, (j + 1) * cw)
            came = jnp.concatenate(
                [crecv[j * cw // 128 + a] for a in range(cw // 128)], axis=1
            ).astype(F32)
            carried = (pref[k, :, cols] + lead[k, 0:1, cols] * came).astype(BF16)
            fc = dotg(reader, carried, 1, 0) * dotg(grow, spread16[:, cols], 1, 0)
            gated = sg[rows, cols].astype(F32) * (y[rows, cols] + fc)
            sq = sq + dotg(unit, (gated * gated).astype(BF16), 1, 1)
            u[rows, cols] = (gated * gaincols[:, cols]).astype(BF16)
        for a in range(BLOCK // rd):
            ss[r0 // rd + a] = sq[:, a * rd : (a + 1) * rd]

    for i in range(X):
        c = lax.rem(chip + 1 + i, X)
        base = c * rows_chip

        def gate_block(b, _):
            gating(base + b * BLOCK)
            return 0

        lax.fori_loop(0, rows_chip // BLOCK, gate_block, 0)
        if i == X - 1:

            def send_ss(o, _):
                ss_copy(o).start()
                return 0

            lax.fori_loop(1, n, send_ss, 0)
        theirs = pl.ds(pl.multiple_of(base + (1 - core) * rd, rd), rd)
        mine = pl.ds(pl.multiple_of(base + core * rd, rd), rd)

        def forward(j):
            to_peer(i, j).wait_recv()
            xsend[i, j] = (acc[j] + precv[i, j].astype(F32)).astype(BF16)
            to_chip(i, j).start()

        def project(j, _):
            cols = pl.ds(pl.multiple_of(j * dc, dc), dc)
            psend[i, j] = dotg(u[theirs, :], w[:, cols], 1, 0).astype(BF16)
            to_peer(i, j).start()
            if i < X - 1:
                @pl.when(j > 0)
                def _():
                    forward(j - 1)
            acc[j] = dotg(u[mine, :], w[:, cols], 1, 0)
            return 0

        lax.fori_loop(0, nc, project, 0)
        if i < X - 1:
            forward(nc - 1)

    sq = ss[m]
    for o in range(1, n):
        ss_copy(o).wait_recv()
        sq = sq + ssrecv[o]
    mean = dotg(sq, jnp.full((8, 128), 0.125, F32), 0, 0, HI) / (ch * n)
    scale = lax.rsqrt(mean + 1e-05)
    scale = jnp.concatenate([scale] * (dc // 128), axis=1)
    for j in range(nc):
        to_peer(X - 1, j).wait_recv()
        value = acc[j] + precv[X - 1, j].astype(F32)
        for i in range(X - 1):
            to_chip(i, j).wait_recv()
            value = value + xrecv[i, j].astype(F32)
        out_ref[:, j * dc : (j + 1) * dc] = (value * scale).astype(BF16)

    for j in range(nc):
        for i in range(X):
            to_peer(i, j).wait_send()
        for i in range(X - 1):
            to_chip(i, j).wait_send()
    for o in range(1, n):
        ss_copy(o).wait_send()

    @pl.when(s < S - 1)
    def _():
        for j in range(pieces):
            chain_copy(j)[0].wait_send()


def body(S, n, x, gate, b, c, step, log_decay, skip, gain, w):
    tok, ch = x.shape
    heads, st, D = step.shape[1], b.shape[1], w.shape[1]
    X, rd, blocks = n // 2, tok // n, tok // BLOCK
    cw = 256 if ch % 256 == 0 else 128
    dc = 512 if D % 512 == 0 else 128
    pieces, nc = ch // 128, D // dc
    cfg = (S, n, tok, ch, heads, D, cw, dc)
    vmem = pl.BlockSpec(memory_space=pltpu.VMEM)
    hbm = pl.BlockSpec(memory_space=pl.ANY)
    V, DMA = pltpu.VMEM, pltpu.SemaphoreType.DMA
    return pl.pallas_call(
        functools.partial(kernel, cfg),
        out_shape=jax.ShapeDtypeStruct((rd, D), BF16),
        in_specs=[vmem, hbm, vmem, vmem, vmem, vmem, vmem, vmem, hbm],
        out_specs=vmem,
        scratch_shapes=[
            V((tok, ch), BF16),
            V(w.shape, BF16),
            V((tok, heads), F32),
            V((8, 128), F32),
            V((blocks, heads, BLOCK), F32),
            V((blocks, st, ch), F32),
            V((blocks + 1, 8, ch), F32),
            V((st, ch), F32),
            V((tok, ch), F32),
            V((tok, ch), BF16),
            V((tok, ch), BF16),
            V((n, 8, rd), F32),
            V((pieces, st, 128), BF16),
            V((pieces, st, 128), BF16),
            V((X, nc, rd, dc), BF16),
            V((X, nc, rd, dc), BF16),
            V((max(X - 1, 1), nc, rd, dc), BF16),
            V((max(X - 1, 1), nc, rd, dc), BF16),
            V((nc, rd, dc), F32),
            V((n, 8, rd), F32),
            DMA((2,)),
            DMA((pieces,)),
            DMA((pieces,)),
            DMA((X, nc)),
            DMA((X, nc)),
            DMA((max(X - 1, 1), nc)),
            DMA((max(X - 1, 1), nc)),
            DMA((n,)),
            DMA((n,)),
        ],
        compiler_params=pltpu.CompilerParams(
            collective_id=0, has_side_effects=True, vmem_limit_bytes=60 * 1024 * 1024
        ),
    )(x, gate, b, c, step.T, log_decay.T, skip[None, :], gain[None, :], w)


def solution(mesh):
    placed = (
        P("seq", "mp"),
        P("seq", "mp"),
        P("seq", None),
        P("seq", None),
        P("seq", "mp"),
        P("seq", "mp"),
        P("mp"),
        P("mp"),
        P("mp", None),
    )
    return jax.shard_map(
        functools.partial(body, mesh.shape["seq"], mesh.shape["mp"]),
        mesh=mesh, in_specs=placed, out_specs=P(("seq", "mp"), None), check_vma=False,
    )
```

time: 256 us -> 82 us (0.32)
  waiting for transfers between devices: 146 us -> 0 us
  Pallas kernels: 0 us -> 78 us
  matrix products: 29.9 us -> 0 us
  other arithmetic: 19.9 us -> 0 us
  blocking collectives: 19.6 us -> 0 us
  local copies, waits for them, and re-layouts: 23.1 us -> 3.74 us
  between operations: 14.4 us -> 0.01 us
    reduce_scatter x1 -> x0, waiting for transfers between devices: 85.6 us -> none  [body(): lax.psum_scatter(jnp.dot(normed, out_weight, preferred_element_type=jnp.f...]
    pallas_call x0 -> x1, Pallas kernels: none -> 78 us  [body(): pl.pallas_call(functools.partial(kernel, cfg), out_shape=jax.ShapeDtypeSt...]
    all_gather x1 -> x0, waiting for transfers between devices: 60.6 us -> none  [carried_in(): everything = jax.tree.map(lambda part: lax.all_gather(part, axis), value)]
    dot_general x5 -> x0, matrix products: 29.9 us -> none  [the longest x1 13.8 us: body(): jnp.dot(normed, out_weight, preferred_element_type=jnp.float32)]
    unnamed x1 -> x0, blocking collectives: 13.9 us -> none
    select_n x8 -> x0, other arithmetic: 9.88 us -> none  [hop(): return jax.tree.map(lambda a, b: jnp.where(reached, a, b), new, before)]
    unnamed x32 -> x1, local copies, waits for them, and re-layouts: 10.4 us -> 2.46 us
    psum x1 -> x0, blocking collectives: 5.67 us -> none  [body(): square_total = lax.psum(jnp.sum(gated * gated, axis=1), 'mp')]
  transfers between devices with their start and end apart: 2 -> 0, of which waited for: 2 -> 0; matrix products, arithmetic and copies ran while one was open for 4% -> 0% of each run, Pallas kernels for 0% -> 0%
where the time goes in v1:
time: 82 us; the launch traced here: 81.8 us
  Pallas kernels  78 us (95%)
  local copies, waits for them, and re-layouts  3.74 us (5%)
    pallas_call x1, Pallas kernels, body(): pl.pallas_call(functools.partial(kernel, cfg), out_shape=jax.ShapeDtypeSt...  78 us
    unnamed x1, local copies, waits for them, and re-layouts  2.46 us

profile of v1, /device:TPU:29, one launch (start us, length us, event | category | flops | bytes accessed | tf_op | source)
XLA Modules:
  0.0 81.8 jit_solution(16978064909218379146)
XLA Ops:
  0.0 1.3 %broadcast_in_dim.7.gain_ref = bf16[1,1280]{1,0:T(2,128)(2,1)} reshape(bf16[1280]{0:T(1024)(128)(2,1)} %param.16) | data formatting | bytes 5120 | tf_op jit(solution)/shard_map/broadcast_in_dim | solution.py:324
  1.3 78.0 %shard_map.91 = bf16[256,2560]{1,0:T(8,128)(2,1)} custom-call(bf16[1024,1280]{1,0:T(8,128)(2,1)} %x_ref.1, bf16[1024,1280]{1,0:T(8,128)(2,1)} %gate_hbm.1, bf16[1024,128]{1,0:T(8,128)(2,1)} %b_ref.1, bf16[1024,128]{1,0:T(8,128)(2,1)} %c_ref.1, f32[20,1024]{1,0:T(8,128)} %bitcast.3, f32[20,1024]{1,0:T(8,128)} %bitcast.4, f32[1,20]{1,0:T(1,128)} %bitcast.5, ...), custom_call_target="tpu_custom_call" | custom-call | tf_op jit(solution)/shard_map/pallas_call | solution.py:285
  79.3 2.5 %copy.11 = bf16[256,2560]{1,0:T(8,128)(2,1)} copy(bf16[256,2560]{1,0:T(8,128)(2,1)} %shard_map.91) | data formatting | bytes 2621440

commit v2 on v1

--- a/solution.py
+++ b/solution.py
@@ -24,8 +24,8 @@
     cfg, x_ref, gate_hbm, b_ref, c_ref, stp_ref, ldt_ref, skip_ref, gain_ref, w_hbm,
     out_ref,
     gate, w, lev, lvs, levt, pref, lead, total, y, sg, u, ss,
-    csend, crecv, psend, precv, xsend, xrecv, acc, ssrecv,
-    load_sem, cs_sem, cr_sem, ps_sem, pr_sem, xs_sem, xr_sem, ss_sem, sr_sem,
+    dpart, gsend, grecv, fsend, prefix, csend, crecv, psend, precv, xsend, xrecv, acc, ssrecv,
+    load_sem, d_sem, gs_sem, gr_sem, fs_sem, fr_sem, cs_sem, cr_sem, ps_sem, pr_sem, xs_sem, xr_sem, ss_sem, sr_sem,
 ):
     S, n, tok, ch, heads, D, cw, dc = cfg
     X, rd, blocks = n // 2, tok // n, tok // BLOCK
@@ -36,6 +36,8 @@
     s, m = lax.axis_index("seq"), lax.axis_index("mp")
     chip, core = m // 2, lax.rem(m, 2)
     peer = chip * 2 + 1 - core
+    odd = lax.rem(s, 2)
+    mate = s + 1 - 2 * odd
 
     load_gate = pltpu.make_async_copy(gate_hbm, gate, load_sem.at[0])
     load_w = pltpu.make_async_copy(w_hbm, w, load_sem.at[1])
@@ -45,9 +47,10 @@
     barrier = pltpu.get_barrier_semaphore()
     for o in range(1, n):
         pl.semaphore_signal(barrier, inc=1, device_id={"mp": lax.rem(m + o, n)})
-    for o in (1, S - 1):
+    for o in (2, S - 2):
         pl.semaphore_signal(barrier, inc=1, device_id={"seq": lax.rem(s + o, S)})
-    pl.semaphore_wait(barrier, n + 1)
+    pl.semaphore_signal(barrier, inc=1, device_id={"seq": mate})
+    pl.semaphore_wait(barrier, n + 2)
 
     spread = (
         lax.broadcasted_iota(jnp.int32, (heads, ch), 1) // hw
@@ -92,49 +95,87 @@
     lead[0] = ones
     lax.fori_loop(0, blocks, states, 0)
 
-    def chain_copy(j):
-        cols = pl.ds(pl.multiple_of(j * 128, 128), 128)
+    n0 = pieces - pieces // 2
+    off, count = odd * n0, jnp.where(odd == 0, n0, pieces - n0)
+    away, left = (1 - odd) * n0, pieces - count
+
+    def remote(src, dst, send, recv, device):
         return pltpu.make_async_remote_copy(
-            src_ref=csend.at[j],
-            dst_ref=crecv.at[j],
-            send_sem=cs_sem.at[j],
-            recv_sem=cr_sem.at[j],
-            device_id={"seq": lax.rem(s + 1, S)},
-        ), cols
-
-    def chain(j, _):
-        copy, cols = chain_copy(j)
-
-        @pl.when(s == 0)
+            src_ref=src, dst_ref=dst, send_sem=send, recv_sem=recv, device_id={"seq": device}
+        )
+
+    decay_copy = remote(lead.at[blocks], dpart, d_sem.at[0], d_sem.at[1], mate)
+
+    def give(j):
+        return remote(gsend.at[j], grecv.at[j], gs_sem.at[j], gr_sem.at[j], mate)
+
+    def hand(j):
+        return remote(csend.at[j], crecv.at[j], cs_sem.at[j], cr_sem.at[j], lax.rem(s + 2, S))
+
+    def back(j):
+        return remote(fsend.at[j], prefix.at[j], fs_sem.at[j], fr_sem.at[j], mate)
+
+    def lanes(j):
+        return pl.ds(pl.multiple_of(j * 128, 128), 128)
+
+    decay_copy.start()
+
+    def give_piece(a, _):
+        j = away + a
+        gsend[j] = total[:, lanes(j)].astype(BF16)
+        give(j).start()
+        return 0
+
+    lax.fori_loop(0, left, give_piece, 0)
+
+    def chain(a):
+        j = off + a
+        cols = lanes(j)
+
+        @pl.when(a == 0)
+        def _():
+            decay_copy.wait_recv()
+
+        give(j).wait_recv()
+
+        @pl.when(s < 2)
         def _():
             crecv[j] = jnp.zeros(crecv.shape[1:], BF16)
 
-        @pl.when(s > 0)
+        @pl.when(s >= 2)
         def _():
-            copy.wait_recv()
-
-        @pl.when(s < S - 1)
+            hand(j).wait_recv()
+
+        even = odd == 0
+        own, other = total[:, cols], grecv[j].astype(F32)
+        d_own, d_other = lead[blocks, 0:1, cols], dpart[0:1, cols]
+        before = crecv[j].astype(F32)
+        middle = jnp.where(even, d_own, d_other) * before + jnp.where(even, own, other)
+
+        @pl.when(s < S - 2)
         def _():
-            after = lead[blocks, 0:1, cols] * crecv[j].astype(F32) + total[:, cols]
+            after = jnp.where(even, d_other, d_own) * middle + jnp.where(even, other, own)
             csend[j] = after.astype(BF16)
-            copy.start()
-
-        return 0
+            hand(j).start()
+
+        fsend[j] = jnp.where(even, middle, before).astype(BF16)
+        back(j).start()
+        prefix[j] = jnp.where(even, before, middle).astype(BF16)
 
     load_gate.wait()
     lane = lax.broadcasted_iota(jnp.int32, (BLOCK, 128), 1)
     skip = dotg(jnp.broadcast_to(skip_ref[...], (8, heads)), spread32, 1, 0, HI)
     half = BLOCK // 2
+    units = blocks * pieces
+    first = units // 4 + (s // 2) * (units - units // 4 - 2 * n0) // max(S // 2 - 1, 1)
 
     def within(k, _):
-        @pl.when(k == (s * blocks) // S)
-        def _():
-            lax.fori_loop(0, pieces, chain, 0)
-
         rows = pl.ds(pl.multiple_of(k * BLOCK, BLOCK), BLOCK)
         inter = jnp.where(ti >= si, dotg(c_ref[rows, :], b_ref[rows, :], 1, 1), 0.0)
+        inter = inter.astype(BF16)
         top, low = inter[:half, :half], inter[half:, :]
         level = lev[rows, :]
+        grow = jnp.exp2(level).astype(BF16)
         for q in range(pieces):
             cols = slice(q * 128, (q + 1) * 128)
             xp = x_ref[rows, cols]
@@ -144,20 +185,33 @@
                 h = q * per + p
                 lt = level[:, h : h + 1]
                 ls = levt[k, h : h + 1, :]
-                g0 = jnp.exp2(jnp.minimum(lt[:half] - ls[:, :half], 0.0)) * top
-                g1 = jnp.exp2(jnp.minimum(lt[half:] - ls, 0.0)) * low
+                g0 = jnp.exp2(jnp.minimum(lt[:half] - ls[:, :half], 0.0).astype(BF16)) * top
+                g1 = jnp.exp2(jnp.minimum(lt[half:] - ls, 0.0).astype(BF16)) * low
                 r = jnp.concatenate(
-                    [dotg(g0.astype(BF16), xp[:half], 1, 0), dotg(g1.astype(BF16), xp, 1, 0)],
+                    [dotg(g0, xp[:half], 1, 0), dotg(g1, xp, 1, 0)],
                     axis=0,
                 )
                 res = r if res is None else jnp.where(lane < p * hw, res, r)
-            y[rows, cols] = mix + res
             v = gate[rows, cols].astype(F32)
-            sg[rows, cols] = (v / (1.0 + jnp.exp(-v))).astype(BF16)
+            silu = v / (1.0 + jnp.exp(-v))
+            y[rows, cols] = (mix + res) * silu
+            sg[rows, cols] = (silu * dotg(grow, spread16[:, cols], 1, 0)).astype(BF16)
+            turn = k * pieces + q - first
+
+            @pl.when((turn >= 0) & (turn < 2 * count) & (lax.rem(turn + units, 2) == 0))
+            def _():
+                chain(turn // 2)
+
         return 0
 
     lax.fori_loop(0, blocks, within, 0)
     load_w.wait()
+
+    def settle(a, _):
+        back(away + a).wait_recv()
+        return 0
+
+    lax.fori_loop(0, left, settle, 0)
 
     def to_peer(i, j):
         return pltpu.make_async_remote_copy(
@@ -187,17 +241,15 @@
     def gating(r0):
         k = r0 // BLOCK
         rows = pl.ds(pl.multiple_of(r0, BLOCK), BLOCK)
-        grow = jnp.exp2(lev[rows, :]).astype(BF16)
         reader = c_ref[rows, :]
         sq = jnp.zeros((8, BLOCK), F32)
         for j in range(ch // cw):
             cols = slice(j * cw, (j + 1) * cw)
             came = jnp.concatenate(
-                [crecv[j * cw // 128 + a] for a in range(cw // 128)], axis=1
+                [prefix[j * cw // 128 + a] for a in range(cw // 128)], axis=1
             ).astype(F32)
             carried = (pref[k, :, cols] + lead[k, 0:1, cols] * came).astype(BF16)
-            fc = dotg(reader, carried, 1, 0) * dotg(grow, spread16[:, cols], 1, 0)
-            gated = sg[rows, cols].astype(F32) * (y[rows, cols] + fc)
+            gated = y[rows, cols] + sg[rows, cols].astype(F32) * dotg(reader, carried, 1, 0)
             sq = sq + dotg(unit, (gated * gated).astype(BF16), 1, 1)
             u[rows, cols] = (gated * gaincols[:, cols]).astype(BF16)
         for a in range(BLOCK // rd):
@@ -265,10 +317,24 @@
     for o in range(1, n):
         ss_copy(o).wait_send()
 
-    @pl.when(s < S - 1)
-    def _():
-        for j in range(pieces):
-            chain_copy(j)[0].wait_send()
+    decay_copy.wait_send()
+
+    def drain_give(a, _):
+        give(away + a).wait_send()
+        return 0
+
+    lax.fori_loop(0, left, drain_give, 0)
+
+    def drain(a, _):
+        back(off + a).wait_send()
+
+        @pl.when(s < S - 2)
+        def _():
+            hand(off + a).wait_send()
+
+        return 0
+
+    lax.fori_loop(0, count, drain, 0)
 
 
 def body(S, n, x, gate, b, c, step, log_decay, skip, gain, w):
@@ -300,6 +366,11 @@
             V((tok, ch), BF16),
             V((tok, ch), BF16),
             V((n, 8, rd), F32),
+            V((8, ch), F32),
+            V((pieces, st, 128), BF16),
+            V((pieces, st, 128), BF16),
+            V((pieces, st, 128), BF16),
+            V((pieces, st, 128), BF16),
             V((pieces, st, 128), BF16),
             V((pieces, st, 128), BF16),
             V((X, nc, rd, dc), BF16),
@@ -309,6 +380,11 @@
             V((nc, rd, dc), F32),
             V((n, 8, rd), F32),
             DMA((2,)),
+            DMA((2,)),
+            DMA((pieces,)),
+            DMA((pieces,)),
+            DMA((pieces,)),
+            DMA((pieces,)),
             DMA((pieces,)),
             DMA((pieces,)),
             DMA((X, nc)),

time: 82 us -> 71.3 us (0.87)
  Pallas kernels: 78 us -> 67.2 us
    pallas_call x1, Pallas kernels: 78 us -> 67.2 us  [body(): pl.pallas_call(functools.partial(kernel, cfg), out_shape=jax.ShapeDtypeSt...]
where the time goes in v2:
time: 71.3 us; the launch traced here: 71 us
  Pallas kernels  67.2 us (94%)
  local copies, waits for them, and re-layouts  3.74 us (5%)
    pallas_call x1, Pallas kernels, body(): pl.pallas_call(functools.partial(kernel, cfg), out_shape=jax.ShapeDtypeSt...  67.2 us
    unnamed x1, local copies, waits for them, and re-layouts  2.46 us

profile of v2, /device:TPU:29, one launch (start us, length us, event | category | flops | bytes accessed | tf_op | source)
XLA Modules:
  0.0 71.0 jit_solution(7901863727932659288)
XLA Ops:
  0.0 1.3 %broadcast_in_dim.7.gain_ref = bf16[1,1280]{1,0:T(2,128)(2,1)} reshape(bf16[1280]{0:T(1024)(128)(2,1)} %param.16) | data formatting | bytes 5120 | tf_op jit(solution)/shard_map/broadcast_in_dim | solution.py:400
  1.3 67.2 %shard_map.91 = bf16[256,2560]{1,0:T(8,128)(2,1)} custom-call(bf16[1024,1280]{1,0:T(8,128)(2,1)} %x_ref.1, bf16[1024,1280]{1,0:T(8,128)(2,1)} %gate_hbm.1, bf16[1024,128]{1,0:T(8,128)(2,1)} %b_ref.1, bf16[1024,128]{1,0:T(8,128)(2,1)} %c_ref.1, f32[20,1024]{1,0:T(8,128)} %bitcast.3, f32[20,1024]{1,0:T(8,128)} %bitcast.4, f32[1,20]{1,0:T(1,128)} %bitcast.5, ...), custom_call_target="tpu_custom_call" | custom-call | tf_op jit(solution)/shard_map/pallas_call | solution.py:351
  68.5 2.5 %copy.11 = bf16[256,2560]{1,0:T(8,128)(2,1)} copy(bf16[256,2560]{1,0:T(8,128)(2,1)} %shard_map.91) | data formatting | bytes 2621440
